TPU v7x, 128 devices: a whole 4x4x4 slice. The times are simulated.
128 devices in a mesh: replica: 2 (over core), fsdp: 16 (over y, x), tensor: 4 (over z).
Axes of the slice: x: 4, y: 4, z: 4, core: 2. Of those that a mesh axis runs over, the one named last changes fastest.
Arguments:
- grads: bfloat16 [2, 2, 4096, 14336], P('replica', None, 'fsdp', 'tensor'), may hold values from -6 to 6
- momentum: bfloat16 [2, 4096, 14336], P(None, 'fsdp', 'tensor'), may hold values from -50 to 50, as said below
- basis: bfloat16 [2, 14336, 512], P(None, 'tensor'), may hold values from -0.046875 to 0.046875
Outputs:
- momentum_new: bfloat16 [2, 4096, 14336], P(None, 'fsdp', 'tensor')
- update: bfloat16 [2, 4096, 14336], P(None, 'fsdp', 'tensor')
- basis_new: bfloat16 [2, 14336, 512], P(None, 'tensor')
Inputs may be any that keep to these rules, and one draw needn't show every extreme that they name: `momentum`: entries are finite.
All inputs are finite; a program needn't handle non-finite values.
Results may differ from a plain program's by a relative error of at most 0.028.
Values may be sent and summed in bfloat16 or wider, within the bound.
A program may use at most 128 MiB of HBM per device.

v0:
```python
import functools
import math
import jax
import jax.numpy as jnp
from jax import lax
from jax.sharding import Mesh
from jax.sharding import PartitionSpec as P

FEATURES = 4096
UNITS = 14336
RANK = 512
FSDP = ("fsdp_0", "fsdp_1")
REPLICA_FSDP_TENSOR = ("replica", "fsdp_0", "fsdp_1", "tensor")
REPLICA_FSDP = ("replica", "fsdp_0", "fsdp_1")
momentum_decay = 0.95


def from_everyone(x, axis):
    size = lax.axis_size(axis)
    return lax.all_to_all(jnp.broadcast_to(x[None], (size, *x.shape)), axis, 0, 0, tiled=True)


def of_everyone(x, axis):
    everything = from_everyone(x, axis)
    return jnp.sum(everything.astype(jnp.float32), axis=0)


def in_blocks(x, dim, size):
    before, after = (x.shape[:dim], x.shape[dim + 1 :])
    return jnp.moveaxis(x.reshape(*before, size, -1, *after), dim, 0)


def piece_ends(length, count):
    unit = 8 if length >= 8 * count else 1
    return [length // unit * k // count * unit for k in range(1, count)]


def own_block(pieces, axes, turns):
    dims = [lax.axis_size(a) for a in axes]
    pieces = pieces.reshape(*dims, *pieces.shape[1:])
    pieces = pieces.transpose(*turns, *range(len(axes), pieces.ndim))
    pieces = pieces.reshape(-1, *pieces.shape[len(axes) :])
    for k in turns:
        pieces = lax.psum_scatter(pieces, axes[k], scatter_dimension=0, tiled=True)
    return pieces[0]


def spread_scatter(x, axes, dim):
    pieces = in_blocks(x, dim, lax.axis_size(axes))
    cut = max(range(1, max(2, pieces.ndim - 1)), key=lambda d: pieces.shape[d])
    count, done = (len(axes), [])
    for initial, section in enumerate(
        jnp.split(pieces, piece_ends(pieces.shape[cut], count), axis=cut)
    ):
        if section.size:
            turns = [(initial + k) % count for k in range(count)]
            done.append(own_block(section, axes, turns))
    return jnp.concatenate(done, axis=cut - 1)


def over_axes(x, axes):
    return functools.reduce(lax.psum, axes, x)


def total_of_pieces(x, axis):
    return lax.all_gather(x, axis).astype(jnp.float32).sum(0)


def orthonormal(projected, factor):

    def solve_one(lower_mat, rows_mat):
        return jax.scipy.linalg.solve_triangular(lower_mat, rows_mat.T, lower=True).T

    return jax.vmap(solve_one)(factor, projected).astype(jnp.bfloat16)


def power_step(total_grad, moment, right):
    blended = (moment.astype(jnp.float32) + total_grad).astype(jnp.bfloat16)
    partial_value = jnp.einsum("wmc,wcr->wmr", blended, right, preferred_element_type=jnp.float32)
    projected = of_everyone(partial_value.astype(jnp.bfloat16), "tensor").astype(jnp.float32)
    gram_local = jnp.einsum(
        "wmr,wms->wrs", projected, projected, preferred_element_type=jnp.float32
    )
    gram_matrix = lax.psum(gram_local.astype(jnp.bfloat16), FSDP).astype(jnp.float32)
    factor = jnp.linalg.cholesky(gram_matrix)
    left_basis = orthonormal(projected, factor)
    half = blended.shape[2] // lax.axis_size("replica")
    offset = lax.axis_index("replica") * half
    kept_half = half // lax.axis_size(FSDP)
    columns = lax.dynamic_slice_in_dim(blended, offset, kept_half * lax.axis_size(FSDP), 2)
    back_piece = spread_scatter(
        jnp.einsum("wmc,wmr->cwr", columns, left_basis, preferred_element_type=jnp.float32).astype(
            jnp.bfloat16
        ),
        FSDP,
        0,
    ).astype(jnp.float32)
    squares = over_axes(jnp.sum(back_piece * back_piece, axis=0), REPLICA_FSDP_TENSOR)
    back_b = back_piece.astype(jnp.bfloat16)
    right_rows = lax.all_gather(back_b, REPLICA_FSDP, axis=0, tiled=True)
    inverse = 1.0 / (jnp.sqrt(squares) + 1e-06)
    normed = (right_rows.astype(jnp.float32) * inverse[None, :, :]).astype(jnp.bfloat16)
    feedback = jnp.einsum(
        "wmr,cwr->wmc", left_basis, right_rows, preferred_element_type=jnp.float32
    )
    momentum_new = (blended.astype(jnp.float32) - (1.0 - momentum_decay) * feedback).astype(
        jnp.bfloat16
    )
    scale = math.sqrt(FEATURES * UNITS / RANK)
    update = (
        scale * jnp.einsum("wmr,cwr->wmc", left_basis, normed, preferred_element_type=jnp.float32)
    ).astype(jnp.bfloat16)
    basis_new = jnp.transpose(normed, (1, 0, 2))
    return (momentum_new, update, basis_new)


def summed_grads(grads):
    return total_of_pieces(grads[0].astype(jnp.float32).astype(jnp.bfloat16), "replica").astype(
        jnp.float32
    )


def shards(grads, momentum, basis):
    return power_step(summed_grads(grads), momentum, basis)


def solution(mesh):
    torus = Mesh(
        mesh.devices.reshape(mesh.shape["replica"], 4, 4, mesh.shape["tensor"]),
        ("replica", "fsdp_0", "fsdp_1", "tensor"),
    )
    return jax.shard_map(
        shards,
        mesh=torus,
        in_specs=(
            P("replica", None, FSDP, "tensor"),
            P(None, FSDP, "tensor"),
            P(None, "tensor", None),
        ),
        out_specs=(P(None, FSDP, "tensor"), P(None, FSDP, "tensor"), P(None, "tensor", None)),
        check_vma=False,
    )
```

profile of v0, /device:TPU:1, one launch (start us, length us, event | category | flops | bytes accessed | tf_op | source)
XLA Modules:
  0.0 627.0 jit_solution(4297394936807727248)
XLA Ops:
  7.9 26.3 %all-gather.3.cloned.1.call-done = bf16[2,2,256,3584]{3,2,1,0:T(8,128)(2,1)} async-done(((bf16[1,2,256,3584]{3,2,1,0:T(8,128)(2,1)}), bf16[2,2,256,3584]{3,2,1,0:T(8,128)(2,1)}) %all-gather.3.cloned.1.call-update) | async-done | bytes 7340048 | tf_op jit(solution)/shard_map/all_gather | solution.py:66
  34.3 5.3 convert_reduce_fusion
  40.7 6.5 %convolution_convert_fusion.2 = bf16[2,256,512]{2,1,0:T(8,128)(2,1)S(1)} fusion(bf16[2,256,3584]{2,1,0:T(8,128)(2,1)S(1)} %add_convert_fusion, bf16[2,3584,512]{2,1,0:T(8,128)(2,1)} %param.5), kind=kOutput, calls=%fused_computation.16 | convolution fusion | flops 1879310336 | bytes 11534336 | tf_op jit(solution)/shard_map/wmc,wcr->wmr/dot_general | solution.py:79
  47.4 30.0 %all_to_all.5 = bf16[4,2,256,512]{3,2,1,0:T(8,128)(2,1)S(1)} all-to-all(bf16[4,2,256,512]{3,2,1,0:T(8,128)(2,1)S(1)} %broadcast_in_dim.4), channel_id=1, replica_groups=mesh['replica'=2,'fsdp_0'=4,'fsdp_1'=4,'tensor'=4] {'tensor'}, dimensions={0} | all-to-all | bytes 4194304 | tf_op jit(solution)/shard_map/all_to_all | solution.py:20
  81.2 83.7 %all-reduce.3.cloned.1.call-done = bf16[2,512,512]{1,2,0:T(8,128)(2,1)} async-done(((bf16[2,512,512]{1,2,0:T(8,128)(2,1)}), bf16[2,512,512]{1,2,0:T(8,128)(2,1)}) %all-reduce.3.cloned.1.call-update) | async-done | bytes 1048592 | tf_op jit(solution)/shard_map/psum | solution.py:84
  168.1 23.5 %custom-call.35 = f32[2,128,128]{2,1,0:T(8,128)S(1)} custom-call(f32[2,128,128]{2,1,0:T(8,128)S(1)} %cholesky.274), custom_call_target="Cholesky" | custom-call | tf_op jit(solution)/shard_map/jit(cholesky)/cholesky | solution.py:85
  191.6 19.7 %custom-call.36 = f32[2,1,128,128]{2,3,1,0:T(8,128)S(1)} custom-call(f32[2,1,128,128]{3,2,1,0:T(8,128)S(1)} %select_bitcast_fusion.2), custom_call_target="InvertDiagBlocksLowerTriangular" | custom-call | tf_op jit(solution)/shard_map/jit(cholesky)/cholesky | solution.py:85
  214.6 23.5 %custom-call.37 = f32[2,128,128]{2,1,0:T(8,128)S(1)} custom-call(f32[2,128,128]{2,1,0:T(8,128)S(1)} %cholesky.278), custom_call_target="Cholesky" | custom-call | tf_op jit(solution)/shard_map/jit(cholesky)/cholesky | solution.py:85
  238.1 19.8 %custom-call.38 = f32[2,1,128,128]{2,3,1,0:T(8,128)S(1)} custom-call(f32[2,1,128,128]{3,2,1,0:T(8,128)S(1)} %get-tuple-element.30), custom_call_target="InvertDiagBlocksLowerTriangular" | custom-call | tf_op jit(solution)/shard_map/jit(cholesky)/cholesky | solution.py:85
  259.9 23.5 %custom-call.39 = f32[2,128,128]{2,1,0:T(8,128)S(1)} custom-call(f32[2,128,128]{2,1,0:T(8,128)S(1)} %cholesky.283), custom_call_target="Cholesky" | custom-call | tf_op jit(solution)/shard_map/jit(cholesky)/cholesky | solution.py:85
  283.4 19.7 %custom-call.40 = f32[2,1,128,128]{2,3,1,0:T(8,128)S(1)} custom-call(f32[2,1,128,128]{3,2,1,0:T(8,128)S(1)} %get-tuple-element.28), custom_call_target="InvertDiagBlocksLowerTriangular" | custom-call | tf_op jit(solution)/shard_map/jit(cholesky)/cholesky | solution.py:85
  304.9 23.7 %custom-call.41 = f32[2,128,128]{2,1,0:T(8,128)S(1)} custom-call(f32[2,128,128]{2,1,0:T(8,128)S(1)} %convolution_subtract_fusion.5), custom_call_target="Cholesky" | custom-call | tf_op jit(solution)/shard_map/jit(cholesky)/cholesky | solution.py:85
  330.7 14.5 %while.1 = (s32[]{:T(128)}, f32[2,512,512]{2,1,0:T(8,128)}, s32[4,2]{0,1:T(2,128)S(1)}, f32[4,2,128,128]{3,2,0,1:T(8,128)}, s32[]{:T(128)}) while((s32[]{:T(128)}, f32[2,512,512]{2,1,0:T(8,128)}, s32[4,2]{0,1:T(2,128)S(1)}, f32[4,2,128,128]{3,2,0,1:T(8,128)}, s32[]{:T(128)}) %tuple.36), condition=%wide.while_cond, body=%wide.while_body.sunk | while | flops 2 | bytes 263277 | solution.py:72
  331.4 3.0 bitcast_dynamic-update-slice_fusion.2
  335.0 3.0 bitcast_dynamic-update-slice_fusion.2
  338.6 3.0 bitcast_dynamic-update-slice_fusion.2
  342.3 2.9 bitcast_dynamic-update-slice_fusion.2
  345.2 79.4 %custom-call.42 = f32[2,4,128,128]{2,3,1,0:T(8,128)S(1)} custom-call(f32[2,4,128,128]{3,2,1,0:T(8,128)} %bitcast.91), custom_call_target="InvertDiagBlocksLowerTriangular" | custom-call | tf_op jit(solution)/shard_map/vmap(jit(_solve_triangular))/triangular_solve | solution.py:72
  430.9 3.0 fusion.1
  433.9 5.9 copy.77
  445.3 26.8 %reduce-scatter.9.cloned.1.call-done = bf16[4,56,2,512]{3,1,2,0:T(8,128)(2,1)} async-done(((bf16[16,56,2,512]{3,1,2,0:T(8,128)(2,1)}), bf16[4,56,2,512]{3,1,2,0:T(8,128)(2,1)}) %reduce-scatter.9.cloned.1.call-update) | async-done | bytes 458768 | tf_op jit(solution)/shard_map/reduce_scatter | solution.py:44
  472.2 30.1 %reduce-scatter.5.cloned.1.call-done = bf16[4,56,2,512]{3,1,2,0:T(8,128)(2,1)} async-done(((bf16[16,56,2,512]{3,1,2,0:T(8,128)(2,1)}), bf16[4,56,2,512]{3,1,2,0:T(8,128)(2,1)}) %reduce-scatter.5.cloned.1.call-update) | async-done | bytes 458768 | tf_op jit(solution)/shard_map/reduce_scatter | solution.py:44
  502.4 21.0 %reduce-scatter.11.cloned.1.call-done = bf16[1,56,2,512]{3,1,2,0:T(8,128)(2,1)} async-done(((bf16[4,56,2,512]{3,1,2,0:T(8,128)(2,1)}), bf16[1,56,2,512]{3,1,2,0:T(8,128)(2,1)}) %reduce-scatter.11.cloned.1.call-update) | async-done | bytes 114704 | tf_op jit(solution)/shard_map/reduce_scatter | solution.py:44
  523.4 23.3 %reduce-scatter.7.cloned.1.call-done = bf16[1,56,2,512]{3,1,2,0:T(8,128)(2,1)} async-done(((bf16[4,56,2,512]{3,1,2,0:T(8,128)(2,1)}), bf16[1,56,2,512]{3,1,2,0:T(8,128)(2,1)}) %reduce-scatter.7.cloned.1.call-update) | async-done | bytes 114704 | tf_op jit(solution)/shard_map/reduce_scatter | solution.py:44
  549.5 5.1 psum.36
  554.6 8.4 %psum.37 = f32[2,512]{1,0:T(2,128)S(1)} all-reduce(f32[2,512]{1,0:T(2,128)S(1)} %psum.36), channel_id=1, replica_groups=mesh['replica'=2,'fsdp_0'=4,'fsdp_1'=4,'tensor'=4] {'fsdp_0'}, use_global_device_ids=true, to_apply=%region_17.18 | all-reduce | flops 1024 | bytes 8192 | tf_op jit(solution)/shard_map/psum | solution.py:62
  563.0 6.5 %psum.38 = f32[2,512]{1,0:T(2,128)S(1)} all-reduce(f32[2,512]{1,0:T(2,128)S(1)} %psum.37), channel_id=1, replica_groups=mesh['replica'=2,'fsdp_0'=4,'fsdp_1'=4,'tensor'=4] {'fsdp_1'}, use_global_device_ids=true, to_apply=%region_18.19 | all-reduce | flops 1024 | bytes 8192 | tf_op jit(solution)/shard_map/psum | solution.py:62
  569.5 9.2 %psum.39 = f32[2,512]{1,0:T(2,128)S(1)} all-reduce(f32[2,512]{1,0:T(2,128)S(1)} %psum.38), channel_id=1, replica_groups=mesh['replica'=2,'fsdp_0'=4,'fsdp_1'=4,'tensor'=4] {'tensor'}, use_global_device_ids=true, to_apply=%region_19.20 | all-reduce | flops 1024 | bytes 8192 | tf_op jit(solution)/shard_map/psum | solution.py:62
  578.8 24.0 %all-gather.5.cloned.1.call-done = bf16[3584,2,512]{2,0,1:T(8,128)(2,1)} async-done(((bf16[112,2,512]{2,0,1:T(8,128)(2,1)}), bf16[3584,2,512]{2,0,1:T(8,128)(2,1)}) %all-gather.5.cloned.1.call-update) | async-done | bytes 7340048 | tf_op jit(solution)/shard_map/all_gather | solution.py:100
  602.8 8.3 %subtract_convert_fusion = bf16[2,256,3584]{2,1,0:T(8,128)(2,1)} fusion(bf16[2,256,3584]{2,1,0:T(8,128)(2,1)} %copy-done, bf16[3584,2,512]{2,0,1:T(8,128)(2,1)} %all-gather.5.cloned.1.call-done, bf16[2,128,256]{2,1,0:T(8,128)(2,1)S(1)} %convolution_convert_fusion.3, bf16[2,128,256]{2,1,0:T(8,128)(2,1)S(1)} %get-tuple-element.34, ...), kind=kOutput, calls=%fused_computation.5 | convolution fusion | flops 1888485376 | bytes 15204352 | tf_op jit(solution)/shard_map/wmr,cwr->wmc/dot_general | solution.py:103
  611.1 4.3 multiply_convert_fusion.1
  615.4 4.5 fusion
  (80 shorter events, 35.4 us)
Async XLA Ops:
  7.2 27.1 %all-gather.3.cloned.1.call-start = ((), (), s32[]{:S(2)}) async-start(), calls=%async_computation.5 | async-start | bytes 11010048 | tf_op jit(solution)/shard_map/all_gather | solution.py:66
  7.9 157.0 %all-reduce.3.cloned.1.call-start = ((), (), s32[]{:S(2)}) async-start(), calls=%async_computation.6 | async-start | bytes 2097152 | tf_op jit(solution)/shard_map/psum | solution.py:84
  34.3 5.3 copy-start.6
  40.7 6.5 %copy-start = (bf16[2,256,3584]{2,1,0:T(8,128)(2,1)}, bf16[2,256,3584]{2,1,0:T(8,128)(2,1)S(1)}, u32[]{:S(2)}) copy-start(bf16[2,256,3584]{2,1,0:T(8,128)(2,1)S(1)} %add_convert_fusion) | copy-start | bytes 11010052
  79.1 393.0 %reduce-scatter.9.cloned.1.call-start = ((), (), s32[]{:S(2)}) async-start(), calls=%async_computation.9 | async-start | bytes 2293760 | tf_op jit(solution)/shard_map/reduce_scatter | solution.py:44
  164.9 1.6 copy-start.4
  166.8 1.3 copy-start.3
  328.9 95.7 %copy-start.5 = (f32[2,256,512]{1,2,0:T(8,128)S(1)}, f32[2,256,512]{1,2,0:T(8,128)}, u32[]{:S(2)}) copy-start(f32[2,256,512]{1,2,0:T(8,128)} %copy.72) | copy-start | bytes 3145732
  426.8 4.1 copy-start.1
  443.7 58.6 %reduce-scatter.5.cloned.1.call-start = ((), (), s32[]{:S(2)}) async-start(), calls=%async_computation.7 | async-start | bytes 2293760 | tf_op jit(solution)/shard_map/reduce_scatter | solution.py:44
  445.3 78.1 %reduce-scatter.11.cloned.1.call-start = ((), (), s32[]{:S(2)}) async-start(), calls=%async_computation.10 | async-start | bytes 573440 | tf_op jit(solution)/shard_map/reduce_scatter | solution.py:44
  472.2 74.6 %reduce-scatter.7.cloned.1.call-start = ((), (), s32[]{:S(2)}) async-start(), calls=%async_computation.8 | async-start | bytes 573440 | tf_op jit(solution)/shard_map/reduce_scatter | solution.py:44
  502.4 100.4 %all-gather.5.cloned.1.call-start = ((), (), s32[]{:S(2)}) async-start(), calls=%async_computation.11 | async-start | bytes 7569408 | tf_op jit(solution)/shard_map/all_gather | solution.py:100
  602.8 8.3 %copy-start.2 = (bf16[3584,2,512]{2,0,1:T(8,128)(2,1)S(1)}, bf16[3584,2,512]{2,0,1:T(8,128)(2,1)}, u32[]{:S(2)}) copy-start(bf16[3584,2,512]{2,0,1:T(8,128)(2,1)} %all-gather.5.cloned.1.call-done) | copy-start | bytes 22020100
Sparse Core Ops, SparseCore 0:
  9.6 24.6 all-gather.2
  79.3 85.5 all-reduce.2
  443.9 28.2 reduce-scatter.8
  475.0 27.3 reduce-scatter.4
  504.6 18.7 reduce-scatter.10
  525.7 21.0 reduce-scatter.6
  549.6 53.1 all-gather.4
where the time goes:
time: 632 us; the launch traced here: 627 us
  other arithmetic  249 us (39%)
  waiting for transfers between devices  236 us (37%)
  blocking collectives  59.2 us (9%)
  matrix products  36.4 us (6%)
  local copies, waits for them, and re-layouts  30.5 us (5%)
  between operations  14.8 us (2%)
    another operation x16, other arithmetic, power_step(): factor = jnp.linalg.cholesky(gram_matrix)  154 us
    reduce_scatter x4, waiting for transfers between devices, own_block(): pieces = lax.psum_scatter(pieces, axes[k], scatter_dimension=0, tiled=True)  101 us
    psum x1, waiting for transfers between devices, power_step(): lax.psum(gram_local.astype(jnp.bfloat16), FSDP).astype(jnp.float32)  83.7 us
    another operation x4, other arithmetic, solve_one(): jax.scipy.linalg.solve_triangular(lower_mat, rows_mat.T, lower=True)  81.2 us
    all_to_all x1, blocking collectives, from_everyone(): lax.all_to_all(jnp.broadcast_to(x[None], (size, *x.shape)), axis, 0, 0, t...  30 us
    psum x4, blocking collectives, over_axes(): return functools.reduce(lax.psum, axes, x)  29.3 us
    all_gather x1, waiting for transfers between devices, total_of_pieces(): return lax.all_gather(x, axis).astype(jnp.float32).sum(0)  26.3 us
    all_gather x1, waiting for transfers between devices, power_step(): right_rows = lax.all_gather(back_b, REPLICA_FSDP, axis=0, tiled=True)  24 us
  transfers between devices with their start and end apart: 7, of which 7 were waited for; matrix products, arithmetic and copies ran while one was open for 1% of the time, Pallas kernels for 0%

commit v1 on v0

--- a/solution.py
+++ b/solution.py
@@ -81,7 +81,9 @@
     gram_local = jnp.einsum(
         "wmr,wms->wrs", projected, projected, preferred_element_type=jnp.float32
     )
-    gram_matrix = lax.psum(gram_local.astype(jnp.bfloat16), FSDP).astype(jnp.float32)
+    gram_matrix = lax.psum(lax.psum(gram_local.astype(jnp.bfloat16), "fsdp_0"), "fsdp_1").astype(
+        jnp.float32
+    )
     factor = jnp.linalg.cholesky(gram_matrix)
     left_basis = orthonormal(projected, factor)
     half = blended.shape[2] // lax.axis_size("replica")

time: 632 us -> 642 us (1.016)
  waiting for transfers between devices: 236 us -> 246 us
    psum x1 -> x2, waiting for transfers between devices: 83.7 us -> 91.6 us  [the longest x1 47.3 us: power_step(): lax.psum(lax.psum(gram_local.astype(jnp.bfloat16), 'fsdp_0'), 'fsdp_1')]
  transfers between devices with their start and end apart: 7 -> 8, of which waited for: 7 -> 8; matrix products, arithmetic and copies ran while one was open for 1% -> 1% of each run, Pallas kernels for 0% -> 0%
where the time goes in v1:
time: 642 us; the launch traced here: 637 us
  other arithmetic  249 us (39%)
  waiting for transfers between devices  246 us (38%)
  blocking collectives  59.2 us (9%)
  matrix products  36.4 us (6%)
  local copies, waits for them, and re-layouts  30.5 us (5%)
  between operations  14.8 us (2%)
    another operation x16, other arithmetic, power_step(): factor = jnp.linalg.cholesky(gram_matrix)  154 us
    reduce_scatter x4, waiting for transfers between devices, own_block(): pieces = lax.psum_scatter(pieces, axes[k], scatter_dimension=0, tiled=True)  103 us
    another operation x4, other arithmetic, solve_one(): jax.scipy.linalg.solve_triangular(lower_mat, rows_mat.T, lower=True)  81.2 us
    psum x1, waiting for transfers between devices, power_step(): lax.psum(lax.psum(gram_local.astype(jnp.bfloat16), 'fsdp_0'), 'fsdp_1')  47.3 us
    psum x1, waiting for transfers between devices, power_step(): lax.psum(gram_local.astype(jnp.bfloat16), 'fsdp_0')  44.3 us
    all_to_all x1, blocking collectives, from_everyone(): lax.all_to_all(jnp.broadcast_to(x[None], (size, *x.shape)), axis, 0, 0, t...  30 us
    psum x4, blocking collectives, over_axes(): return functools.reduce(lax.psum, axes, x)  29.2 us
    all_gather x1, waiting for transfers between devices, total_of_pieces(): return lax.all_gather(x, axis).astype(jnp.float32).sum(0)  26.3 us
  transfers between devices with their start and end apart: 8, of which 8 were waited for; matrix products, arithmetic and copies ran while one was open for 1% of the time, Pallas kernels for 0%

profile of v1, /device:TPU:1, one launch (start us, length us, event | category | flops | bytes accessed | tf_op | source)
XLA Modules:
  0.0 637.2 jit_solution(10419069845722586621)
XLA Ops:
  7.9 26.3 %all-gather.3.cloned.1.call-done = bf16[2,2,256,3584]{3,2,1,0:T(8,128)(2,1)} async-done(((bf16[1,2,256,3584]{3,2,1,0:T(8,128)(2,1)}), bf16[2,2,256,3584]{3,2,1,0:T(8,128)(2,1)}) %all-gather.3.cloned.1.call-update) | async-done | bytes 7340048 | tf_op jit(solution)/shard_map/all_gather | solution.py:66
  34.3 5.3 convert_reduce_fusion
  40.7 6.5 %convolution_convert_fusion.2 = bf16[2,256,512]{2,1,0:T(8,128)(2,1)S(1)} fusion(bf16[2,256,3584]{2,1,0:T(8,128)(2,1)S(1)} %add_convert_fusion, bf16[2,3584,512]{2,1,0:T(8,128)(2,1)} %param.5), kind=kOutput, calls=%fused_computation.16 | convolution fusion | flops 1879310336 | bytes 11534336 | tf_op jit(solution)/shard_map/wmc,wcr->wmr/dot_general | solution.py:79
  47.4 30.0 %all_to_all.5 = bf16[4,2,256,512]{3,2,1,0:T(8,128)(2,1)S(1)} all-to-all(bf16[4,2,256,512]{3,2,1,0:T(8,128)(2,1)S(1)} %broadcast_in_dim.4), channel_id=1, replica_groups=mesh['replica'=2,'fsdp_0'=4,'fsdp_1'=4,'tensor'=4] {'tensor'}, dimensions={0} | all-to-all | bytes 4194304 | tf_op jit(solution)/shard_map/all_to_all | solution.py:20
  79.2 44.3 %all-reduce.4.cloned.1.call-done = bf16[2,512,512]{1,2,0:T(8,128)(2,1)} async-done(((bf16[2,512,512]{1,2,0:T(8,128)(2,1)}), bf16[2,512,512]{1,2,0:T(8,128)(2,1)}) %all-reduce.4.cloned.1.call-update) | async-done | bytes 1048592 | tf_op jit(solution)/shard_map/psum | solution.py:84
  125.6 47.3 %all-reduce.6.cloned.1.call-done = bf16[2,512,512]{1,2,0:T(8,128)(2,1)} async-done(((bf16[2,512,512]{1,2,0:T(8,128)(2,1)}), bf16[2,512,512]{1,2,0:T(8,128)(2,1)}) %all-reduce.6.cloned.1.call-update) | async-done | bytes 1048592 | tf_op jit(solution)/shard_map/psum | solution.py:84
  176.2 23.5 %custom-call.35 = f32[2,128,128]{2,1,0:T(8,128)S(1)} custom-call(f32[2,128,128]{2,1,0:T(8,128)S(1)} %cholesky.274), custom_call_target="Cholesky" | custom-call | tf_op jit(solution)/shard_map/jit(cholesky)/cholesky | solution.py:87
  199.7 19.7 %custom-call.36 = f32[2,1,128,128]{2,3,1,0:T(8,128)S(1)} custom-call(f32[2,1,128,128]{3,2,1,0:T(8,128)S(1)} %select_bitcast_fusion.2), custom_call_target="InvertDiagBlocksLowerTriangular" | custom-call | tf_op jit(solution)/shard_map/jit(cholesky)/cholesky | solution.py:87
  222.6 23.5 %custom-call.37 = f32[2,128,128]{2,1,0:T(8,128)S(1)} custom-call(f32[2,128,128]{2,1,0:T(8,128)S(1)} %cholesky.278), custom_call_target="Cholesky" | custom-call | tf_op jit(solution)/shard_map/jit(cholesky)/cholesky | solution.py:87
  246.1 19.8 %custom-call.38 = f32[2,1,128,128]{2,3,1,0:T(8,128)S(1)} custom-call(f32[2,1,128,128]{3,2,1,0:T(8,128)S(1)} %get-tuple-element.30), custom_call_target="InvertDiagBlocksLowerTriangular" | custom-call | tf_op jit(solution)/shard_map/jit(cholesky)/cholesky | solution.py:87
  267.9 23.5 %custom-call.39 = f32[2,128,128]{2,1,0:T(8,128)S(1)} custom-call(f32[2,128,128]{2,1,0:T(8,128)S(1)} %cholesky.283), custom_call_target="Cholesky" | custom-call | tf_op jit(solution)/shard_map/jit(cholesky)/cholesky | solution.py:87
  291.4 19.7 %custom-call.40 = f32[2,1,128,128]{2,3,1,0:T(8,128)S(1)} custom-call(f32[2,1,128,128]{3,2,1,0:T(8,128)S(1)} %get-tuple-element.28), custom_call_target="InvertDiagBlocksLowerTriangular" | custom-call | tf_op jit(solution)/shard_map/jit(cholesky)/cholesky | solution.py:87
  312.9 23.7 %custom-call.41 = f32[2,128,128]{2,1,0:T(8,128)S(1)} custom-call(f32[2,128,128]{2,1,0:T(8,128)S(1)} %convolution_subtract_fusion.5), custom_call_target="Cholesky" | custom-call | tf_op jit(solution)/shard_map/jit(cholesky)/cholesky | solution.py:87
  338.7 14.5 %while.1 = (s32[]{:T(128)}, f32[2,512,512]{2,1,0:T(8,128)}, s32[4,2]{0,1:T(2,128)S(1)}, f32[4,2,128,128]{3,2,0,1:T(8,128)}, s32[]{:T(128)}) while((s32[]{:T(128)}, f32[2,512,512]{2,1,0:T(8,128)}, s32[4,2]{0,1:T(2,128)S(1)}, f32[4,2,128,128]{3,2,0,1:T(8,128)}, s32[]{:T(128)}) %tuple.36), condition=%wide.while_cond, body=%wide.while_body.sunk | while | flops 2 | bytes 263277 | solution.py:72
  339.4 3.0 bitcast_dynamic-update-slice_fusion.2
  343.0 3.0 bitcast_dynamic-update-slice_fusion.2
  346.7 3.0 bitcast_dynamic-update-slice_fusion.2
  353.3 79.4 %custom-call.42 = f32[2,4,128,128]{2,3,1,0:T(8,128)S(1)} custom-call(f32[2,4,128,128]{3,2,1,0:T(8,128)} %bitcast.91), custom_call_target="InvertDiagBlocksLowerTriangular" | custom-call | tf_op jit(solution)/shard_map/vmap(jit(_solve_triangular))/triangular_solve | solution.py:72
  439.0 3.0 fusion.1
  441.9 5.9 copy.77
  453.4 28.8 %reduce-scatter.9.cloned.1.call-done = bf16[4,56,2,512]{3,1,2,0:T(8,128)(2,1)} async-done(((bf16[16,56,2,512]{3,1,2,0:T(8,128)(2,1)}), bf16[4,56,2,512]{3,1,2,0:T(8,128)(2,1)}) %reduce-scatter.9.cloned.1.call-update) | async-done | bytes 458768 | tf_op jit(solution)/shard_map/reduce_scatter | solution.py:44
  482.2 30.1 %reduce-scatter.5.cloned.1.call-done = bf16[4,56,2,512]{3,1,2,0:T(8,128)(2,1)} async-done(((bf16[16,56,2,512]{3,1,2,0:T(8,128)(2,1)}), bf16[4,56,2,512]{3,1,2,0:T(8,128)(2,1)}) %reduce-scatter.5.cloned.1.call-update) | async-done | bytes 458768 | tf_op jit(solution)/shard_map/reduce_scatter | solution.py:44
  512.4 21.0 %reduce-scatter.11.cloned.1.call-done = bf16[1,56,2,512]{3,1,2,0:T(8,128)(2,1)} async-done(((bf16[4,56,2,512]{3,1,2,0:T(8,128)(2,1)}), bf16[1,56,2,512]{3,1,2,0:T(8,128)(2,1)}) %reduce-scatter.11.cloned.1.call-update) | async-done | bytes 114704 | tf_op jit(solution)/shard_map/reduce_scatter | solution.py:44
  533.5 23.5 %reduce-scatter.7.cloned.1.call-done = bf16[1,56,2,512]{3,1,2,0:T(8,128)(2,1)} async-done(((bf16[4,56,2,512]{3,1,2,0:T(8,128)(2,1)}), bf16[1,56,2,512]{3,1,2,0:T(8,128)(2,1)}) %reduce-scatter.7.cloned.1.call-update) | async-done | bytes 114704 | tf_op jit(solution)/shard_map/reduce_scatter | solution.py:44
  559.6 5.1 psum.44
  564.8 8.4 %psum.45 = f32[2,512]{1,0:T(2,128)S(1)} all-reduce(f32[2,512]{1,0:T(2,128)S(1)} %psum.44), channel_id=1, replica_groups=mesh['replica'=2,'fsdp_0'=4,'fsdp_1'=4,'tensor'=4] {'fsdp_0'}, use_global_device_ids=true, to_apply=%region_18.19 | all-reduce | flops 1024 | bytes 8192 | tf_op jit(solution)/shard_map/psum | solution.py:62
  573.2 6.4 %psum.46 = f32[2,512]{1,0:T(2,128)S(1)} all-reduce(f32[2,512]{1,0:T(2,128)S(1)} %psum.45), channel_id=1, replica_groups=mesh['replica'=2,'fsdp_0'=4,'fsdp_1'=4,'tensor'=4] {'fsdp_1'}, use_global_device_ids=true, to_apply=%region_19.20 | all-reduce | flops 1024 | bytes 8192 | tf_op jit(solution)/shard_map/psum | solution.py:62
  579.6 9.2 %psum.47 = f32[2,512]{1,0:T(2,128)S(1)} all-reduce(f32[2,512]{1,0:T(2,128)S(1)} %psum.46), channel_id=1, replica_groups=mesh['replica'=2,'fsdp_0'=4,'fsdp_1'=4,'tensor'=4] {'tensor'}, use_global_device_ids=true, to_apply=%region_20.21 | all-reduce | flops 1024 | bytes 8192 | tf_op jit(solution)/shard_map/psum | solution.py:62
  588.9 24.0 %all-gather.5.cloned.1.call-done = bf16[3584,2,512]{2,0,1:T(8,128)(2,1)} async-done(((bf16[112,2,512]{2,0,1:T(8,128)(2,1)}), bf16[3584,2,512]{2,0,1:T(8,128)(2,1)}) %all-gather.5.cloned.1.call-update) | async-done | bytes 7340048 | tf_op jit(solution)/shard_map/all_gather | solution.py:102
  612.9 8.3 %subtract_convert_fusion = bf16[2,256,3584]{2,1,0:T(8,128)(2,1)} fusion(bf16[2,256,3584]{2,1,0:T(8,128)(2,1)} %copy-done, bf16[3584,2,512]{2,0,1:T(8,128)(2,1)} %all-gather.5.cloned.1.call-done, bf16[2,128,256]{2,1,0:T(8,128)(2,1)S(1)} %convolution_convert_fusion.3, bf16[2,128,256]{2,1,0:T(8,128)(2,1)S(1)} %get-tuple-element.34, ...), kind=kOutput, calls=%fused_computation.5 | convolution fusion | flops 1888485376 | bytes 15204352 | tf_op jit(solution)/shard_map/wmr,cwr->wmc/dot_general | solution.py:105
  621.3 4.3 multiply_convert_fusion.1
  625.5 4.5 fusion
  (83 shorter events, 38.4 us)
Async XLA Ops:
  7.2 27.1 %all-gather.3.cloned.1.call-start = ((), (), s32[]{:S(2)}) async-start(), calls=%async_computation.5 | async-start | bytes 11010048 | tf_op jit(solution)/shard_map/all_gather | solution.py:66
  7.9 115.6 %all-reduce.4.cloned.1.call-start = ((), (), s32[]{:S(2)}) async-start(), calls=%async_computation.6 | async-start | bytes 2097152 | tf_op jit(solution)/shard_map/psum | solution.py:84
  34.3 5.3 copy-start.6
  40.7 6.5 %copy-start = (bf16[2,256,3584]{2,1,0:T(8,128)(2,1)}, bf16[2,256,3584]{2,1,0:T(8,128)(2,1)S(1)}, u32[]{:S(2)}) copy-start(bf16[2,256,3584]{2,1,0:T(8,128)(2,1)S(1)} %add_convert_fusion) | copy-start | bytes 11010052
  79.1 93.8 %all-reduce.6.cloned.1.call-start = ((), (), s32[]{:S(2)}) async-start(), calls=%async_computation.7 | async-start | bytes 2097152 | tf_op jit(solution)/shard_map/psum | solution.py:84
  123.5 358.6 %reduce-scatter.9.cloned.1.call-start = ((), (), s32[]{:S(2)}) async-start(), calls=%async_computation.10 | async-start | bytes 2293760 | tf_op jit(solution)/shard_map/reduce_scatter | solution.py:44
  172.9 1.6 copy-start.4
  174.8 1.3 copy-start.3
  337.0 95.7 %copy-start.5 = (f32[2,256,512]{1,2,0:T(8,128)S(1)}, f32[2,256,512]{1,2,0:T(8,128)}, u32[]{:S(2)}) copy-start(f32[2,256,512]{1,2,0:T(8,128)} %copy.72) | copy-start | bytes 3145732
  434.9 4.1 copy-start.1
  451.8 60.6 %reduce-scatter.5.cloned.1.call-start = ((), (), s32[]{:S(2)}) async-start(), calls=%async_computation.8 | async-start | bytes 2293760 | tf_op jit(solution)/shard_map/reduce_scatter | solution.py:44
  453.3 80.1 %reduce-scatter.11.cloned.1.call-start = ((), (), s32[]{:S(2)}) async-start(), calls=%async_computation.11 | async-start | bytes 573440 | tf_op jit(solution)/shard_map/reduce_scatter | solution.py:44
  482.2 74.8 %reduce-scatter.7.cloned.1.call-start = ((), (), s32[]{:S(2)}) async-start(), calls=%async_computation.9 | async-start | bytes 573440 | tf_op jit(solution)/shard_map/reduce_scatter | solution.py:44
  512.4 100.5 %all-gather.5.cloned.1.call-start = ((), (), s32[]{:S(2)}) async-start(), calls=%async_computation.12 | async-start | bytes 7569408 | tf_op jit(solution)/shard_map/all_gather | solution.py:102
  612.9 8.3 %copy-start.2 = (bf16[3584,2,512]{2,0,1:T(8,128)(2,1)S(1)}, bf16[3584,2,512]{2,0,1:T(8,128)(2,1)}, u32[]{:S(2)}) copy-start(bf16[3584,2,512]{2,0,1:T(8,128)(2,1)} %all-gather.5.cloned.1.call-done) | copy-start | bytes 22020100
Sparse Core Ops, SparseCore 0:
  9.6 24.6 all-gather.2
  79.3 44.2 all-reduce.3
  125.9 46.9 all-reduce.5
  451.9 30.1 reduce-scatter.8
  485.0 27.3 reduce-scatter.4
  514.6 18.8 reduce-scatter.10
  535.9 21.0 reduce-scatter.6
  559.8 53.0 all-gather.4
